TPU v7x, 32 devices: a whole 2x2x4 slice. The times are simulated.
32 devices in a mesh: seq: 8 (over z, x), fsdp: 4 (over y, core).
Axes of the slice: x: 2, y: 2, z: 4, core: 2. Of those that a mesh axis runs over, the one named last changes fastest.
Arguments:
- tokens: bfloat16 [4, 1024, 2048], P('fsdp', 'seq'), may hold values from -6 to 6
- cotangent: bfloat16 [4, 1024, 2048], P('fsdp', 'seq'), may hold values from -6 to 6
- routes: int32 [4, 1024, 8], P('fsdp', 'seq'), may hold values from 0 to 63, all different within a row; in each aligned block of 128 rows (0 to 127, 128 to 255, ..., all dimensions but the last counted through in order) at most 32 rows name the same one
- norm1_gain: bfloat16 [2048], P(('seq', 'fsdp')), may hold values from 0.099609375 to 1.8984375
- query_weight: bfloat16 [2048, 2048], P(('seq', 'fsdp')), may hold values from -0.125 to 0.125
- key_weight: bfloat16 [2048, 2048], P(('seq', 'fsdp')), may hold values from -0.125 to 0.125
- value_weight: bfloat16 [2048, 2048], P(('seq', 'fsdp')), may hold values from -0.125 to 0.125
- output_weight: bfloat16 [2048, 2048], P(('seq', 'fsdp')), may hold values from -2 to 2
- norm2_gain: bfloat16 [2048], P(('seq', 'fsdp')), may hold values from 0.099609375 to 1.8984375
- router_weight: bfloat16 [2048, 64], P(('seq', 'fsdp')), may hold values from -0.125 to 0.125
- expert_gate: bfloat16 [128, 2048, 512], P(('seq', 'fsdp')), may hold values from -0.125 to 0.125
- expert_up: bfloat16 [128, 2048, 512], P(('seq', 'fsdp')), may hold values from -0.125 to 0.125
- expert_down: bfloat16 [128, 512, 2048], P(('seq', 'fsdp')), may hold values from -0.75 to 0.75
Outputs:
- block_out: bfloat16 [4, 1024, 2048], P('fsdp', 'seq')
- input_grad: float32 [4, 1024, 2048], P('fsdp', 'seq')
- norm1_gain_grad: float32 [2048], P(('seq', 'fsdp'))
- query_weight_grad: float32 [2048, 2048], P(('seq', 'fsdp'))
- key_weight_grad: float32 [2048, 2048], P(('seq', 'fsdp'))
- value_weight_grad: float32 [2048, 2048], P(('seq', 'fsdp'))
- output_weight_grad: float32 [2048, 2048], P(('seq', 'fsdp'))
- norm2_gain_grad: float32 [2048], P(('seq', 'fsdp'))
- router_weight_grad: float32 [2048, 64], P(('seq', 'fsdp'))
- expert_gate_grad: float32 [128, 2048, 512], P(('seq', 'fsdp'))
- expert_up_grad: float32 [128, 2048, 512], P(('seq', 'fsdp'))
- expert_down_grad: float32 [128, 512, 2048], P(('seq', 'fsdp'))
Inputs may be any that keep to these rules, and one draw needn't show every extreme that they name: `routes`: each row names 8 different experts. Among the 128 rows of one device (aligned blocks of the flattened sequences) no expert is named more than 32 times, and in every draw some expert is named exactly 32 times in some block; every expert is named somewhere.
All inputs are finite; a program needn't handle non-finite values.
Results may differ from a plain program's by a relative error of at most 0.02.
Values may be sent and summed in bfloat16 or wider, within the bound.
A program may use at most 448 MiB of HBM per device.

v0:
```python
import jax
import jax.numpy as jnp
from jax import lax
from jax.sharding import PartitionSpec as P

H = 16
HD = 128
SPLIT = 2
AXES = ("seq", "fsdp")
epsilon = 1e-06
rope_base = 50000.0
bf16 = jnp.bfloat16
f32 = jnp.float32


def norm_rows(values, scales):
    mean_sq = jnp.mean(values * values, axis=-1, keepdims=True)
    return values * lax.rsqrt(mean_sq + epsilon) * scales


def rope_tables(positions, head_dim):
    half_dim = head_dim // 2
    frequency = rope_base ** (-(2.0 * jnp.arange(half_dim, dtype=f32)) / head_dim)
    angles = positions.astype(f32)[:, None] * frequency[None, :]
    return (jnp.cos(angles), jnp.sin(angles))


def rotate(values, cosine, sine_tab, inverse):
    half_dim = values.shape[-1] // 2
    low_half = values[..., :half_dim]
    high_half = values[..., half_dim:]
    cos_rows = cosine[:, None, :]
    sin_rows = -sine_tab[:, None, :] if inverse else sine_tab[:, None, :]
    return jnp.concatenate(
        [low_half * cos_rows - high_half * sin_rows, high_half * cos_rows + low_half * sin_rows],
        axis=-1,
    )


def route_weights(logits, chosen):
    expo = jnp.exp(logits)
    probability = expo / jnp.sum(expo, axis=-1, keepdims=True)
    experts = jnp.arange(logits.shape[1], dtype=jnp.int32)
    match = (chosen[:, :, None] == experts).astype(f32)
    picked = jnp.sum(match * probability[:, None, :], axis=-1)
    return picked / jnp.sum(picked, axis=-1, keepdims=True)


def mm(left, right):
    return jnp.dot(left, right, preferred_element_type=f32)


def mm_tn(left, right):
    return lax.dot_general(left, right, (((0,), (0,)), ((), ())), preferred_element_type=f32)


def mm_nt(left, right):
    return lax.dot_general(left, right, (((1,), (1,)), ((), ())), preferred_element_type=f32)


def ein(spec, *args):
    return jnp.einsum(spec, *args, preferred_element_type=f32)


def body(
    tokens,
    cotangent,
    routes,
    norm1_gain,
    query_weight,
    key_weight,
    value_weight,
    output_weight,
    norm2_gain,
    router_weight,
    expert_gate,
    expert_up,
    expert_down,
):
    n_seq = lax.axis_size("seq")
    n_fsdp = lax.axis_size("fsdp")
    n_dev = n_seq * n_fsdp
    seq_at = lax.axis_index("seq")
    dev_at = seq_at * n_fsdp + lax.axis_index("fsdp")
    tok_rows, width = (tokens.shape[1], tokens.shape[2])
    length = tok_rows * n_seq
    heads = H // n_seq
    cols = heads * HD
    shard = query_weight.shape[0]
    experts = router_weight.shape[1]
    top_k = routes.shape[2]
    capacity = tok_rows * top_k // experts * 2
    pieces = expert_gate.shape[0]
    n_loc = max(1, pieces // SPLIT)
    per_loc = pieces // n_loc
    first_expert = dev_at * pieces // SPLIT
    x_own = tokens[0]
    cot_own = cotangent[0]
    chosen = routes[0]
    routes_all = lax.all_gather(chosen, AXES, axis=0, tiled=True)
    x_seq = lax.all_gather(x_own, "seq", axis=0, tiled=True)
    small = jnp.concatenate(
        [
            router_weight,
            norm1_gain[:, None],
            norm2_gain[:, None],
            jnp.zeros((shard, 128 - experts - 2), bf16),
        ],
        axis=1,
    )
    blocks = jnp.concatenate(
        [
            query_weight.reshape(shard, n_seq, cols),
            key_weight.reshape(shard, n_seq, cols),
            value_weight.reshape(shard, n_seq, cols),
            jnp.broadcast_to(small[:, None, :], (shard, n_seq, 128)),
        ],
        axis=2,
    ).transpose(1, 0, 2)
    moved = lax.all_to_all(blocks, "seq", split_axis=0, concat_axis=0, tiled=True)
    packed = lax.all_gather(moved, "fsdp", axis=1).reshape(width, 3 * cols + 128)
    w_qkv = packed[:, : 3 * cols]
    router_full = packed[:, 3 * cols : 3 * cols + experts]
    gain_in = packed[:, 3 * cols + experts].astype(f32)
    gain_mid = packed[:, 3 * cols + experts + 1].astype(f32)
    out_full = lax.all_gather(output_weight, AXES, axis=0, tiled=True)
    out_rows = lax.dynamic_slice_in_dim(out_full, seq_at * cols, cols, 0)
    cot_all = lax.all_gather(cot_own, AXES, axis=0, tiled=True)
    cosine, sine_tab = rope_tables(jnp.arange(length, dtype=jnp.int32), HD)
    normed_in = norm_rows(x_seq.astype(f32), gain_in).astype(bf16)
    qkv = mm(normed_in, w_qkv)
    q = rotate(qkv[:, :cols].reshape(length, heads, HD), cosine, sine_tab, False).astype(bf16)
    k = rotate(qkv[:, cols : 2 * cols].reshape(length, heads, HD), cosine, sine_tab, False).astype(
        bf16
    )
    v = qkv[:, 2 * cols :].astype(bf16).reshape(length, heads, HD)
    scale = HD ** (-0.5)
    scores = ein("qhd,khd->hqk", q, k) * scale
    totals = jnp.log(jnp.sum(jnp.exp(scores), axis=-1))
    probs = jnp.exp(scores - totals[..., None])
    attn_heads = ein("hqk,khd->qhd", probs.astype(bf16), v).astype(bf16)
    attn_flat = attn_heads.reshape(length, cols)
    attn_rows = lax.all_to_all(attn_flat, "seq", split_axis=0, concat_axis=1, tiled=True)
    x_own32 = x_own.astype(f32)
    residual = x_own32 + mm(attn_rows, out_full)
    normed_mid = norm_rows(residual, gain_mid).astype(bf16)
    x_all = lax.all_gather(normed_mid, AXES, axis=0, tiled=True)
    logits_all = mm(x_all, router_full)
    w_all = route_weights(logits_all, routes_all)
    local = first_expert + jnp.arange(n_loc, dtype=jnp.int32)
    match = routes_all.reshape(n_dev, tok_rows, top_k)[:, None] == local[None, :, None, None]
    hit = jnp.any(match, axis=-1)
    w_hit = jnp.sum(jnp.where(match, w_all.reshape(n_dev, 1, tok_rows, top_k), 0.0), axis=-1)
    tri = (jnp.arange(tok_rows)[:, None] <= jnp.arange(tok_rows)[None, :]).astype(bf16)
    place = ein("bet,tu->beu", hit.astype(bf16), tri).astype(jnp.int32) - 1
    slots = jnp.arange(capacity, dtype=jnp.int32)
    pick = hit[:, :, None, :] & (place[:, :, None, :] == slots[None, None, :, None])
    one = pick.astype(bf16)
    w_slot = jnp.sum(jnp.where(pick, w_hit[:, :, None, :], 0.0), axis=-1)
    rows_of = lambda a: ein("best,btd->ebsd", one, a.reshape(n_dev, tok_rows, width)).reshape(
        n_loc, n_dev * capacity, width
    )
    rows_in = rows_of(x_all).astype(bf16)
    rows_cot = rows_of(cot_all)
    w_rows = w_slot.transpose(1, 0, 2).reshape(n_loc, n_dev * capacity, 1)
    rows_grad = (w_rows * rows_cot).astype(bf16)
    gate = expert_gate.reshape(n_loc, per_loc, width, -1)
    up = expert_up.reshape(n_loc, per_loc, width, -1)
    down = expert_down.reshape(n_loc, per_loc, -1, width)
    pre_gate = ein("erd,epdf->eprf", rows_in, gate)
    pre_up = ein("erd,epdf->eprf", rows_in, up)
    sig = jax.nn.sigmoid(pre_gate)
    active = pre_gate * sig
    hidden = (active * pre_up).astype(bf16)
    hidden_grad = ein("erd,epfd->eprf", rows_grad, down)
    gate_grad = (hidden_grad * pre_up * sig * (1.0 + pre_gate * (1.0 - sig))).astype(bf16)
    up_grad = (hidden_grad * active).astype(bf16)
    back = ein("eprf,epdf->erd", gate_grad, gate) + ein("eprf,epdf->erd", up_grad, up)
    out = ein("eprf,epfd->erd", hidden, down)
    w_back = jnp.sum(rows_cot * out, axis=-1)
    spread = (
        lambda a: ein("best,ebsd->btd", one, a.astype(bf16).reshape(n_loc, n_dev, capacity, width))
        .astype(bf16)
        .reshape(n_dev * tok_rows, width)
    )
    back_own = lax.psum_scatter(spread(back), AXES, scatter_dimension=0, tiled=True)
    w_tok = jnp.sum(
        jnp.where(pick, w_back.reshape(n_loc, n_dev, capacity).transpose(1, 0, 2)[..., None], 0.0),
        axis=2,
    )
    w_parts = lax.all_to_all(w_tok, AXES, split_axis=0, concat_axis=0, tiled=True)
    w_by_expert = w_parts.reshape(experts, n_dev * n_loc // experts, tok_rows).sum(axis=1)
    own_match = (chosen[:, :, None] == jnp.arange(experts, dtype=jnp.int32)).astype(f32)
    weight_grad = jnp.sum(own_match * w_by_expert.T[:, None, :], axis=-1)
    moe_own = lax.psum_scatter(spread(w_rows * out), AXES, scatter_dimension=0, tiled=True)
    block_out = (residual + moe_own.astype(f32)).astype(bf16)
    down_grad = ein("eprf,erd->epfd", hidden, rows_grad).reshape(expert_down.shape)
    gate_weight_grad = ein("erd,eprf->epdf", rows_in, gate_grad).reshape(expert_gate.shape)
    up_weight_grad = ein("erd,eprf->epdf", rows_in, up_grad).reshape(expert_up.shape)
    logits = mm(normed_mid, router_full)
    _, route_back = jax.vjp(lambda values: route_weights(values, chosen), logits)
    logit_grad = route_back(weight_grad)[0].astype(bf16)
    normed_total = back_own.astype(f32) + mm_nt(logit_grad, router_full)
    logit_all = lax.all_gather(logit_grad, AXES, axis=0, tiled=True)
    x_cols = lax.dynamic_slice_in_dim(x_all, dev_at * shard, shard, 1)
    grad_router = mm_tn(x_cols, logit_all)
    cot32 = cot_own.astype(f32)
    _, norm_back = jax.vjp(norm_rows, residual, gain_mid)
    resid_part, gain_two = norm_back(normed_total)
    resid_grad = cot32 + resid_part
    resid_seq = lax.all_gather(resid_grad.astype(bf16), "seq", axis=0, tiled=True)
    grad_out_rows = mm_tn(attn_flat, resid_seq)
    grad_output = lax.psum_scatter(grad_out_rows, "fsdp", scatter_dimension=0, tiled=True)
    attn_grad = mm_nt(resid_seq, out_rows).astype(bf16).reshape(length, heads, HD)
    delta = jnp.sum(attn_grad.astype(f32) * attn_heads.astype(f32), axis=-1)
    v_grad = ein("hqk,qhd->khd", probs.astype(bf16), attn_grad).astype(bf16)
    p_grad = ein("qhd,khd->hqk", attn_grad, v)
    s_grad = (probs * (p_grad - delta.T[:, :, None]) * scale).astype(bf16)
    q_grad = ein("hqk,khd->qhd", s_grad, k).astype(bf16)
    k_grad = ein("hqk,qhd->khd", s_grad, q).astype(bf16)
    q_rows = rotate(q_grad.astype(f32), cosine, sine_tab, True).astype(bf16)
    k_rows = rotate(k_grad.astype(f32), cosine, sine_tab, True).astype(bf16)
    d_qkv = jnp.concatenate([a.reshape(length, cols) for a in (q_rows, k_rows, v_grad)], axis=1)
    in_part = mm_nt(d_qkv, w_qkv).astype(bf16)
    normed_in_grad = lax.psum_scatter(in_part, "seq", scatter_dimension=0, tiled=True).astype(f32)
    _, norm_back_in = jax.vjp(norm_rows, x_own32, gain_in)
    input_part, gain_one = norm_back_in(normed_in_grad)
    input_grad = resid_grad + input_part
    grad_qkv = mm_tn(normed_in, d_qkv).reshape(n_seq, n_fsdp, shard, 3 * cols)
    grad_qkv = lax.psum_scatter(grad_qkv, "fsdp", scatter_dimension=1, tiled=False)
    grad_qkv = lax.all_to_all(grad_qkv, "seq", split_axis=0, concat_axis=0, tiled=True)
    grad_qkv = (
        grad_qkv.reshape(n_seq, shard, 3, cols).transpose(2, 1, 0, 3).reshape(3, shard, width)
    )
    gains = lax.psum_scatter(
        jnp.stack([gain_one, gain_two]).reshape(2, n_dev, shard),
        AXES,
        scatter_dimension=1,
        tiled=False,
    )
    return (
        block_out[None],
        input_grad[None],
        gains[0],
        grad_qkv[0],
        grad_qkv[1],
        grad_qkv[2],
        grad_output,
        gains[1],
        grad_router,
        gate_weight_grad,
        up_weight_grad,
        down_grad,
    )


def solution(mesh):
    rows3 = P("fsdp", "seq", None)
    flat = P(AXES)
    two = P(AXES, None)
    three = P(AXES, None, None)
    return jax.shard_map(
        body,
        mesh=mesh,
        in_specs=(rows3, rows3, rows3, flat, two, two, two, two, flat, two, three, three, three),
        out_specs=(rows3, rows3, flat, two, two, two, two, flat, two, three, three, three),
        check_vma=False,
    )
```

profile of v0, /device:TPU:0, one launch (start us, length us, event | category | flops | bytes accessed | tf_op | source)
XLA Modules:
  0.0 1324.9 jit_solution(16863959521056442889)
XLA Ops:
  12.9 30.4 %all_to_all.34 = bf16[8,64,896]{2,1,0:T(8,128)(2,1)S(1)} all-to-all(bf16[8,64,896]{2,1,0:T(8,128)(2,1)S(1)} %copy.233), channel_id=1, replica_groups=mesh['seq'=8,'fsdp'=4] {'seq'}, dimensions={0} | all-to-all | bytes 1835008 | tf_op jit(solution)/shard_map/all_to_all | solution.py:120
  46.9 3.1 fusion.80
  50.0 25.2 %all-gather.19.cloned.1.call-done = bf16[8,256,896]{2,0,1:T(8,128)(2,1)} async-done(((bf16[8,64,896]{2,0,1:T(8,128)(2,1)}), bf16[8,256,896]{2,0,1:T(8,128)(2,1)}) %all-gather.19.cloned.1.call-update) | async-done | bytes 3670032 | tf_op jit(solution)/shard_map/all_gather | solution.py:121
  75.1 2.6 copy.235
  77.8 1.8 copy-done.4
  80.2 69.8 %all-gather.17.cloned.1.call-done = bf16[1,1024,2048]{2,1,0:T(8,128)(2,1)} async-done(((bf16[1,128,2048]{2,1,0:T(8,128)(2,1)}), bf16[1,1024,2048]{2,1,0:T(8,128)(2,1)}) %all-gather.17.cloned.1.call-update) | async-done | bytes 4194320 | tf_op jit(solution)/shard_map/all_gather | solution.py:101
  150.0 3.1 fusion.5
  153.7 6.6 fusion.30
  164.2 2.3 fusion.95
  166.5 2.4 copy.296
  168.9 2.4 copy.297
  171.2 3.4 subtract_convert_fusion.3
  174.6 9.4 fusion.8
  184.1 4.2 fusion.36
  189.1 28.2 %all_to_all.35 = bf16[8,128,256]{1,2,0:T(8,128)(2,1)S(1)} all-to-all(bf16[8,128,256]{1,2,0:T(8,128)(2,1)S(1)} %copy.241), channel_id=1, replica_groups=mesh['seq'=8,'fsdp'=4] {'seq'}, dimensions={0} | all-to-all | bytes 1048576 | tf_op jit(solution)/shard_map/all_to_all | solution.py:143
  217.3 14.1 %all-gather.11.cloned.1.call-done = bf16[2048,2048]{1,0:T(8,128)(2,1)} async-done(((bf16[64,2048]{1,0:T(8,128)(2,1)}), bf16[2048,2048]{1,0:T(8,128)(2,1)}) %all-gather.11.cloned.1.call-update) | async-done | bytes 8388624 | tf_op jit(solution)/shard_map/all_gather | solution.py:126
  231.4 4.8 multiply_reduce_fusion.3
  238.2 40.8 %all-gather.2 = s32[1,4096,8]{1,2,0:T(8,128)S(1)} all-gather(s32[1,128,8]{1,2,0:T(8,128)S(1)} %copy-done.24), channel_id=4, replica_groups=mesh['seq'=8,'fsdp'=4] {'seq','fsdp'}, dimensions={1}, use_global_device_ids=true | all-gather | bytes 135168 | tf_op jit(solution)/shard_map/all_gather | solution.py:100
  279.3 68.4 %all-gather.21.cloned.1.call-done = bf16[1,4096,2048]{2,1,0:T(8,128)(2,1)} async-done(((bf16[1,128,2048]{2,1,0:T(8,128)(2,1)}), bf16[1,4096,2048]{2,1,0:T(8,128)(2,1)}) %all-gather.21.cloned.1.call-update) | async-done | bytes 16777232 | tf_op jit(solution)/shard_map/all_gather | solution.py:128
  347.7 7.0 convolution_bitcast_fusion
  354.8 6.2 copy.247
  361.0 102.1 %all-gather.13.cloned.1.call-done = bf16[4096,2048]{1,0:T(8,128)(2,1)} async-done(((bf16[128,2048]{1,0:T(8,128)(2,1)}), bf16[4096,2048]{1,0:T(8,128)(2,1)}) %all-gather.13.cloned.1.call-update) | async-done | bytes 16777232 | tf_op jit(solution)/shard_map/all_gather | solution.py:147
  463.0 9.4 convert_bitcast_fusion
  472.4 8.3 copy.245
  480.7 15.8 %fusion.98 = f32[2,1024,2,512]{3,1,2,0:T(8,128)} fusion(bf16[2,1024,2048,1]{2,1,3,0:T(8,128)(2,1)} %bitcast.248, bf16[2,2,2048,512]{3,2,1,0:T(8,128)(2,1)} %bitcast.297), kind=kOutput, calls=%fused_computation.181 | convolution fusion | flops 8589934592 | bytes 25165824 | tf_op jit(solution)/shard_map/erd,epdf->eprf/dot_general | solution.py:62
  496.4 15.0 %fusion.17 = (bf16[2,2,1024,512]{3,2,1,0:T(8,128)(2,1)S(1)}, f32[2,1024,2,512]{3,1,2,0:T(8,128)}) fusion(f32[2,1024,2,512]{3,1,2,0:T(8,128)} %fusion.98, bf16[2,1024,2048,1]{2,1,3,0:T(8,128)(2,1)S(1)} %bitcast.251, bf16[2,2,2048,512]{3,2,1,0:T(8,128)(2,1)} %bitcast.299), kind=kOutput, calls=%fused_computation.31 | convolution fusion | flops 8602517504 | bytes 37748736 | tf_op jit(solution)/shard_map/erd,epdf->eprf/dot_general | solution.py:62
  511.4 19.9 %fusion.3 = (f32[2,1024]{1,0:T(2,128)S(1)}, f32[2,1024,2048,1]{2,1,3,0:T(8,128)}) fusion(f32[2,32,32,2048]{3,2,1,0:T(8,128)} %copy.247, bf16[2,2,1024,512]{3,2,1,0:T(8,128)(2,1)S(1)} %get-tuple-element.133, bf16[2,2,512,2048]{3,2,1,0:T(8,128)(2,1)} %bitcast.295), kind=kOutput, calls=%fused_computation.8 | convolution fusion | flops 8598321152 | bytes 46145536 | tf_op jit(solution)/shard_map/eprf,epfd->erd/dot_general | solution.py:62
  531.4 11.0 fusion.97
  542.6 1.6 select_reduce_fusion
  545.6 17.0 %fusion.2 = (bf16[2,1024,2048]{2,1,0:T(8,128)(2,1)}, bf16[2,1024,2048]{2,1,0:T(8,128)(2,1)}) fusion(f32[2,32,32,2048]{3,2,1,0:T(8,128)} %copy.247, f32[2,1024]{1,0:T(2,128)S(1)} %mul.567, f32[2,1024,2048,1]{2,1,3,0:T(8,128)} %get-tuple-element.136), kind=kLoop, calls=%fused_computation.7 | loop fusion | flops 16777216 | bytes 50339840 | tf_op jit(solution)/shard_map/convert_element_type | solution.py:166
  562.6 18.9 %fusion.16 = (bf16[2,2,1024,512]{3,2,1,0:T(8,128)(2,1)}, bf16[2,2,1024,512]{3,2,1,0:T(8,128)(2,1)S(1)}) fusion(f32[2,1024,2,512]{3,1,2,0:T(8,128)} %fusion.98, f32[2,1024,2,512]{3,1,2,0:T(8,128)} %get-tuple-element.134, bf16[2,2,512,2048]{3,2,1,0:T(8,128)(2,1)} %bitcast.296, bf16[2,1024,2048]{2,1,0:T(8,128)(2,1)} %get-tuple-element.122), kind=kOutput, calls=%fused_computation.29 | convolution fusion | flops 8617197568 | bytes 41943040 | tf_op jit(solution)/shard_map/erd,epfd->eprf/dot_general | solution.py:62
  581.5 16.2 %fusion.99 = f32[2,1024,2048,1]{2,1,3,0:T(8,128)} fusion(bf16[2,2,1024,512]{3,2,1,0:T(8,128)(2,1)S(1)} %get-tuple-element.98, bf16[2,2,2048,512]{3,2,1,0:T(8,128)(2,1)} %bitcast.298), kind=kOutput, calls=%fused_computation.182 | convolution fusion | flops 8589934592 | bytes 29360128 | tf_op jit(solution)/shard_map/eprf,epdf->erd/dot_general | solution.py:62
  597.6 16.9 %fusion.1 = bf16[2,1024,2048]{2,1,0:T(8,128)(2,1)} fusion(f32[2,1024,2048,1]{2,1,3,0:T(8,128)} %fusion.99, bf16[2,2,1024,512]{3,2,1,0:T(8,128)(2,1)} %get-tuple-element.97, bf16[2,2,2048,512]{3,2,1,0:T(8,128)(2,1)} %bitcast.300), kind=kOutput, calls=%fused_computation.4 | convolution fusion | flops 8598323200 | bytes 37748736 | tf_op jit(solution)/shard_map/eprf,epdf->erd/dot_general | solution.py:62
  614.6 10.7 bitcast_convert_fusion
  627.8 2.8 all-to-all-start.2
  630.7 11.0 all-to-all-done.2
  641.9 167.0 %reduce-scatter.8.cloned.1.call-done = bf16[128,2048]{1,0:T(8,128)(2,1)} async-done(((bf16[4096,2048]{1,0:T(8,128)(2,1)}), bf16[128,2048]{1,0:T(8,128)(2,1)}) %reduce-scatter.8.cloned.1.call-update) | async-done | bytes 524304 | tf_op jit(solution)/shard_map/reduce_scatter | solution.py:186
  808.9 1.8 multiply_reduce_fusion
  812.1 74.1 %all-gather.15.cloned.1.call-done = bf16[1024,2048]{1,0:T(8,128)(2,1)} async-done(((bf16[128,2048]{1,0:T(8,128)(2,1)}), bf16[1024,2048]{1,0:T(8,128)(2,1)}) %all-gather.15.cloned.1.call-update) | async-done | bytes 4194320 | tf_op jit(solution)/shard_map/all_gather | solution.py:211
  886.2 4.1 multiply_reduce_fusion.1
  890.3 5.9 fusion.39
  897.6 2.0 fusion.43
  903.2 2.0 copy.260
  906.2 6.8 fusion.47
  913.0 3.4 copy.262
  916.4 8.0 convolution_convert_fusion
  924.5 11.1 bitcast_convert_fusion.1
  937.0 16.9 %fusion.101 = f32[2,2,512,2048]{3,2,1,0:T(8,128)} fusion(bf16[2,2,1024,512]{3,2,1,0:T(8,128)(2,1)} %copy-done.34, bf16[2,1024,2048,1]{2,1,3,0:T(8,128)(2,1)} %bitcast.249), kind=kOutput, calls=%fused_computation.184 | convolution fusion | flops 8589934592 | bytes 29360128 | tf_op jit(solution)/shard_map/erd,eprf->epdf/dot_general | solution.py:62
  953.9 2.6 fusion.100
  956.6 16.5 %fusion.102 = f32[2,2,512,2048]{3,2,1,0:T(8,128)} fusion(bf16[2,2,1024,512]{3,2,1,0:T(8,128)(2,1)} %get-tuple-element.97, bf16[2,1024,2048,1]{2,1,3,0:T(8,128)(2,1)} %bitcast.250), kind=kOutput, calls=%fused_computation.185 | convolution fusion | flops 8589934592 | bytes 29360128 | tf_op jit(solution)/shard_map/erd,eprf->epdf/dot_general | solution.py:62
  973.9 5.7 all-to-all-start.3
  979.7 16.6 %fusion.9 = f32[2,2,512,2048]{3,2,1,0:T(8,128)} fusion(bf16[2,2,1024,512]{3,2,1,0:T(8,128)(2,1)} %copy-done.33, bf16[2,1024,2048]{2,1,0:T(8,128)(2,1)} %get-tuple-element.122), kind=kOutput, calls=%fused_computation.20 | convolution fusion | flops 8589934592 | bytes 29360128 | tf_op jit(solution)/shard_map/eprf,erd->epfd/dot_general | solution.py:62
  996.3 16.4 %copy.269 = f32[4,2048,512]{2,1,0:T(8,128)} copy(f32[4,2048,512]{1,2,0:T(8,128)} %bitcast.240) | data formatting | bytes 33554432
  1012.6 16.5 %copy.270 = f32[4,2048,512]{2,1,0:T(8,128)} copy(f32[4,2048,512]{1,2,0:T(8,128)} %bitcast.241) | data formatting | bytes 33554432
  1029.1 42.9 %all_gather.35 = bf16[4096,64]{0,1:T(8,128)(2,1)S(1)} all-gather(bf16[128,64]{0,1:T(8,128)(2,1)S(1)} %multiply_convert_fusion.2), channel_id=1, replica_groups=mesh['seq'=8,'fsdp'=4] {'seq','fsdp'}, dimensions={0}, use_global_device_ids=true | all-gather | bytes 540672 | tf_op jit(solution)/shard_map/all_gather | solution.py:204
  1072.0 2.6 fusion.57
  1074.6 21.2 %reduce-scatter.10.cloned.1.call-done = bf16[128,2048]{1,0:T(8,128)(2,1)} async-done(((bf16[1024,2048]{1,0:T(8,128)(2,1)}), bf16[128,2048]{1,0:T(8,128)(2,1)}) %reduce-scatter.10.cloned.1.call-update) | async-done | bytes 524304 | tf_op jit(solution)/shard_map/reduce_scatter | solution.py:225
  1095.9 1.6 fusion.51
  1097.6 45.8 %all-reduce = f32[2,32,64]{2,0,1:T(2,128)S(1)} all-reduce(f32[2,32,64]{2,0,1:T(2,128)S(1)} %pad_maximum_fusion.7), channel_id=9, replica_groups=mesh['seq'=8,'fsdp'=4] {'seq','fsdp'}, use_global_device_ids=true, to_apply=%region_27.28.clone | all-reduce | flops 4096 | bytes 32768
  1144.0 138.5 %reduce-scatter.6.cloned.1.call-done = bf16[128,2048]{1,0:T(8,128)(2,1)} async-done(((bf16[4096,2048]{1,0:T(8,128)(2,1)}), bf16[128,2048]{1,0:T(8,128)(2,1)}) %reduce-scatter.6.cloned.1.call-update) | async-done | bytes 524304 | tf_op jit(solution)/shard_map/reduce_scatter | solution.py:195
  1282.5 2.8 fusion.54
  1285.3 2.6 reshape.357
  1288.0 1.5 fusion.93
  1293.2 25.0 %reduce-scatter.14.cloned.1.call-done = f32[64,2048]{1,0:T(8,128)} async-done(((f32[256,2048]{1,0:T(8,128)}), f32[64,2048]{1,0:T(8,128)}) %reduce-scatter.14.cloned.1.call-update) | async-done | bytes 524304 | tf_op jit(solution)/shard_map/reduce_scatter | solution.py:213
  (168 shorter events, 36.0 us)
Async XLA Ops:
  7.2 67.9 %all-gather.19.cloned.1.call-start = ((), (), s32[]{:S(2)}) async-start(), calls=%async_computation.18 | async-start | bytes 4587520 | tf_op jit(solution)/shard_map/all_gather | solution.py:121
  44.7 105.3 %all-gather.17.cloned.1.call-start = ((), (), s32[]{:S(2)}) async-start(), calls=%async_computation.17 | async-start | bytes 4718592 | tf_op jit(solution)/shard_map/all_gather | solution.py:101
  45.5 185.9 %all-gather.11.cloned.1.call-start = ((), (), s32[]{:S(2)}) async-start(), calls=%async_computation.9 | async-start | bytes 8650752 | tf_op jit(solution)/shard_map/all_gather | solution.py:126
  46.2 301.5 %all-gather.21.cloned.1.call-start = ((), (), s32[]{:S(2)}) async-start(), calls=%async_computation.19 | async-start | bytes 17301504 | tf_op jit(solution)/shard_map/all_gather | solution.py:128
  46.8 416.2 %all-gather.13.cloned.1.call-start = ((), (), s32[]{:S(2)}) async-start(), calls=%async_computation.10 | async-start | bytes 17301504 | tf_op jit(solution)/shard_map/all_gather | solution.py:147
  49.9 121.3 %copy-start.6 = (f32[1024,64]{1,0:T(8,128)}, f32[1024,64]{1,0:T(8,128)S(1)}, u32[]{:S(2)}) copy-start(f32[1024,64]{1,0:T(8,128)S(1)} %get-tuple-element.126) | copy-start | bytes 786436
  77.7 1.8 copy-start.4
  80.2 72.9 %copy-start.22 = (f32[2048]{0:T(1024)}, f32[2048]{0:T(1024)S(1)}, u32[]{:S(2)}) copy-start(f32[2048]{0:T(1024)S(1)} %get-tuple-element.85) | copy-start | bytes 24580
  80.2 156.0 %copy-start.20 = (f32[2048]{0:T(1024)}, f32[2048]{0:T(1024)S(1)}, u32[]{:S(2)}) copy-start(f32[2048]{0:T(1024)S(1)} %get-tuple-element.84) | copy-start | bytes 24580
  153.1 0.6 copy-start.28
  160.4 23.6 %copy-start.10 = (bf16[1024,256]{0,1:T(8,128)(2,1)}, bf16[1024,256]{0,1:T(8,128)(2,1)S(1)}, u32[]{:S(2)}) copy-start(bf16[1024,256]{0,1:T(8,128)(2,1)S(1)} %slice.127) | copy-start | bytes 1572868
  184.0 47.4 %copy-start.2 = (bf16[1,128,2048]{2,1,0:T(8,128)(2,1)S(1)}, bf16[1,128,2048]{2,1,0:T(8,128)(2,1)}, u32[]{:S(2)}) copy-start(bf16[1,128,2048]{2,1,0:T(8,128)(2,1)} %param.13) | copy-start | bytes 1572868
  188.2 0.8 copy-start.17
  231.4 6.8 copy-start.24
  236.2 1.0 copy-start
  236.2 42.8 %copy-start.30 = (f32[128]{0:T(128)}, f32[128]{0:T(128)S(1)}, u32[]{:S(2)}) copy-start(f32[128]{0:T(128)S(1)} %get-tuple-element.129) | copy-start | bytes 1540
  236.2 42.8 %copy-start.26 = (f32[128]{0:T(128)}, f32[128]{0:T(128)S(1)}, u32[]{:S(2)}) copy-start(f32[128]{0:T(128)S(1)} %fusion.86) | copy-start | bytes 1540
  238.1 570.7 %reduce-scatter.8.cloned.1.call-start = ((), (), s32[]{:S(2)}) async-start(), calls=%async_computation.12 | async-start | bytes 17301504 | tf_op jit(solution)/shard_map/reduce_scatter | solution.py:186
  480.7 15.8 %copy-start.5 = (bf16[2,32,32,2048]{3,2,1,0:T(8,128)(2,1)S(1)}, bf16[2,32,32,2048]{3,2,1,0:T(8,128)(2,1)}, u32[]{:S(2)}) copy-start(bf16[2,32,32,2048]{3,2,1,0:T(8,128)(2,1)} %copy.245) | copy-start | bytes 25165828
  511.4 19.9 %copy-start.33 = (bf16[2,2,1024,512]{3,2,1,0:T(8,128)(2,1)}, bf16[2,2,1024,512]{3,2,1,0:T(8,128)(2,1)S(1)}, u32[]{:S(2)}) copy-start(bf16[2,2,1024,512]{3,2,1,0:T(8,128)(2,1)S(1)} %get-tuple-element.133) | copy-start | bytes 12582916
  581.5 16.2 %copy-start.34 = (bf16[2,2,1024,512]{3,2,1,0:T(8,128)(2,1)}, bf16[2,2,1024,512]{3,2,1,0:T(8,128)(2,1)S(1)}, u32[]{:S(2)}) copy-start(bf16[2,2,1024,512]{3,2,1,0:T(8,128)(2,1)S(1)} %get-tuple-element.98) | copy-start | bytes 12582916
  625.3 1.0 copy-start.8
  625.3 16.3 %copy-start.25 = (s32[1,128,8]{1,2,0:T(8,128)S(1)}, s32[1,128,8]{1,2,0:T(8,128)}, u32[]{:S(2)}) copy-start(s32[1,128,8]{1,2,0:T(8,128)} %param.15) | copy-start | bytes 12292
  625.3 183.5 %copy-start.1 = (f32[128,2048]{1,0:T(8,128)S(1)}, f32[128,2048]{1,0:T(8,128)}, u32[]{:S(2)}) copy-start(f32[128,2048]{1,0:T(8,128)} %copy-done) | copy-start | bytes 3145732
  625.3 183.5 %copy-start.21 = (f32[2048]{0:T(1024)S(1)}, f32[2048]{0:T(1024)}, u32[]{:S(2)}) copy-start(f32[2048]{0:T(1024)} %copy-done.20) | copy-start | bytes 24580
  625.3 183.5 %copy-start.27 = (f32[128]{0:T(128)S(1)}, f32[128]{0:T(128)}, u32[]{:S(2)}) copy-start(f32[128]{0:T(128)} %copy-done.26) | copy-start | bytes 1540
  625.3 185.3 %copy-start.31 = (f32[128]{0:T(128)S(1)}, f32[128]{0:T(128)}, u32[]{:S(2)}) copy-start(f32[128]{0:T(128)} %copy-done.30) | copy-start | bytes 1540
  625.4 185.3 %copy-start.9 = (bf16[1,128,2048]{2,1,0:T(8,128)(2,1)S(1)}, bf16[1,128,2048]{2,1,0:T(8,128)(2,1)}, u32[]{:S(2)}) copy-start(bf16[1,128,2048]{2,1,0:T(8,128)(2,1)} %param.14) | copy-start | bytes 1572868
  627.8 13.9 %all-to-all-start.2 = ((f32[32,2,128]{2,1,0:T(2,128)}), f32[32,2,128]{2,1,0:T(2,128)S(1)}, u32[]{:S(2)}, u32[]{:S(2)}) async-start(f32[32,2,128]{2,1,0:T(2,128)} %get-tuple-element.92), calls=%async_computation.4 | async-start | bytes 65536 | tf_op jit(solution)/shard_map/all_to_all | solution.py:191
  630.6 255.6 %all-gather.15.cloned.1.call-start = ((), (), s32[]{:S(2)}) async-start(), calls=%async_computation.13 | async-start | bytes 4718592 | tf_op jit(solution)/shard_map/all_gather | solution.py:211
  811.9 162.1 %reduce-scatter.12.cloned.1.call-start = ((), (), s32[]{:S(2)}) async-start(), calls=%async_computation.15 | async-start | bytes 7864320 | tf_op jit(solution)/shard_map/reduce_scatter | solution.py:230
  812.1 84.1 %copy-start.11 = (bf16[1024,256]{0,1:T(8,128)(2,1)S(1)}, bf16[1024,256]{0,1:T(8,128)(2,1)}, u32[]{:S(2)}) copy-start(bf16[1024,256]{0,1:T(8,128)(2,1)} %copy-done.10) | copy-start | bytes 1572868
  886.2 9.9 slice-start
  890.3 5.9 slice-start.1
  896.2 1.4 copy-start.14
  896.2 1.4 copy-start.15
  896.2 3.4 copy-start.12
  896.2 3.4 copy-start.13
  897.6 3.4 copy-start.7
  897.6 3.4 copy-start.16
  899.7 6.6 copy-start.23
  899.7 6.5 copy-start.29
  913.0 3.5 copy-start.19
  916.4 179.5 %reduce-scatter.10.cloned.1.call-start = ((), (), s32[]{:S(2)}) async-start(), calls=%async_computation.14 | async-start | bytes 4718592 | tf_op jit(solution)/shard_map/reduce_scatter | solution.py:225
  924.5 358.0 %reduce-scatter.6.cloned.1.call-start = ((), (), s32[]{:S(2)}) async-start(), calls=%async_computation.11 | async-start | bytes 17301504 | tf_op jit(solution)/shard_map/reduce_scatter | solution.py:195
  935.6 1.2 copy-start.3
  935.6 382.6 %reduce-scatter.14.cloned.1.call-start = ((), (), s32[]{:S(2)}) async-start(), calls=%async_computation.16 | async-start | bytes 2621440 | tf_op jit(solution)/shard_map/reduce_scatter | solution.py:213
  937.0 17.0 %copy-start.18 = (bf16[2,128,1024]{2,1,0:T(8,128)(2,1)S(1)}, bf16[2,128,1024]{2,1,0:T(8,128)(2,1)}, u32[]{:S(2)}) copy-start(bf16[2,128,1024]{2,1,0:T(8,128)(2,1)} %copy-done.17) | copy-start | bytes 1572868
  937.0 17.0 %copy-start.32 = (bf16[1024,2048]{1,0:T(8,128)(2,1)S(1)}, bf16[1024,2048]{1,0:T(8,128)(2,1)}, u32[]{:S(2)}) copy-start(bf16[1024,2048]{1,0:T(8,128)(2,1)} %all-gather.15.cloned.1.call-done) | copy-start | bytes 12582916
  973.9 311.4 %all-to-all-start.3 = ((f32[8,64,768]{2,1,0:T(8,128)}), f32[8,64,768]{2,1,0:T(8,128)}, u32[]{:S(2)}, u32[]{:S(2)}) async-start(f32[8,64,768]{2,1,0:T(8,128)} %bitcast.270), calls=%async_computation.7 | async-start | bytes 3145728 | tf_op jit(solution)/shard_map/all_to_all | solution.py:231
Sparse Core Ops, SparseCore 0:
  44.9 30.1 all-gather.18
  77.2 72.7 all-gather.16
  152.9 78.4 all-gather.10
  234.1 113.5 all-gather.20
  350.5 112.5 all-gather.12
  625.5 183.2 reduce-scatter.7
  812.0 74.2 all-gather.14
  916.5 57.3 reduce-scatter.11
  977.6 118.2 reduce-scatter.9
  1098.0 184.4 reduce-scatter.5
  1285.6 32.5 reduce-scatter.13
where the time goes:
time: 1340 us; the launch traced here: 1320 us
  waiting for transfers between devices  719 us (54%)
  matrix products  265 us (20%)
  blocking collectives  188 us (14%)
  local copies, waits for them, and re-layouts  88.1 us (7%)
  other arithmetic  40.5 us (3%)
  between operations  14.8 us (1%)
    dot_general x19, matrix products, ein(): return jnp.einsum(spec, *args, preferred_element_type=f32)  206 us
    reduce_scatter x1, waiting for transfers between devices, body(): lax.psum_scatter(spread(back), AXES, scatter_dimension=0, tiled=True)  167 us
    reduce_scatter x1, waiting for transfers between devices, body(): lax.psum_scatter(spread(w_rows * out), AXES, scatter_dimension=0, tiled=T...  139 us
    all_gather x1, waiting for transfers between devices, body(): x_all = lax.all_gather(normed_mid, AXES, axis=0, tiled=True)  102 us
    all_gather x1, waiting for transfers between devices, body(): lax.all_gather(resid_grad.astype(bf16), 'seq', axis=0, tiled=True)  74.1 us
    all_gather x1, waiting for transfers between devices, body(): x_seq = lax.all_gather(x_own, 'seq', axis=0, tiled=True)  69.8 us
    all_gather x1, waiting for transfers between devices, body(): cot_all = lax.all_gather(cot_own, AXES, axis=0, tiled=True)  68.4 us
    unnamed x88, local copies, waits for them, and re-layouts  51 us
  transfers between devices with their start and end apart: 13, of which 12 were waited for; matrix products, arithmetic and copies ran while one was open for 14% of the time, Pallas kernels for 0%

commit v1 on v0

--- a/solution.py
+++ b/solution.py
@@ -98,7 +98,12 @@
     cot_own = cotangent[0]
     chosen = routes[0]
     routes_all = lax.all_gather(chosen, AXES, axis=0, tiled=True)
-    x_seq = lax.all_gather(x_own, "seq", axis=0, tiled=True)
+    ring = [x_own]
+    for hop in range(7):
+        ring.append(lax.ppermute(ring[-1], "seq", [(dev, (dev + 1) % 8) for dev in range(8)]))
+    x_seq = jnp.roll(
+        jnp.concatenate(ring[::-1], axis=0), (lax.axis_index("seq") + 1) * ring[0].shape[0], axis=0
+    )
     small = jnp.concatenate(
         [
             router_weight,

time: 1340 us -> 1280 us (0.955); the launches traced: 1320 us -> 1280 us
  waiting for transfers between devices: 719 us -> 669 us
    ppermute x0 -> x7, waiting for transfers between devices: none -> 115 us  [body(): lax.ppermute(ring[-1], 'seq', [(dev, (dev + 1) % 8) for dev in range(8)])]
    all_gather x1 -> x0, waiting for transfers between devices: 69.8 us -> none  [body(): x_seq = lax.all_gather(x_own, 'seq', axis=0, tiled=True)]
    all_gather x1, waiting for transfers between devices: 68.4 us -> 12.5 us  [body(): cot_all = lax.all_gather(cot_own, AXES, axis=0, tiled=True)]
    all_gather x1, waiting for transfers between devices: 25.2 us -> 0.02 us  [body(): lax.all_gather(moved, 'fsdp', axis=1).reshape(width, 3 * cols + 128)]
    all_gather x1, waiting for transfers between devices: 14.1 us -> 0.01 us  [body(): out_full = lax.all_gather(output_weight, AXES, axis=0, tiled=True)]
    unnamed x88 -> x113, local copies, waits for them, and re-layouts: 51 us -> 60.4 us
  transfers between devices with their start and end apart: 13 -> 19, of which waited for: 12 -> 16; matrix products, arithmetic and copies ran while one was open for 14% -> 15% of each run, Pallas kernels for 0% -> 0%
where the time goes in v1:
time: 1280 us
  waiting for transfers between devices  669 us (52%)
  matrix products  262 us (20%)
  blocking collectives  187 us (15%)
  local copies, waits for them, and re-layouts  97.5 us (8%)
  other arithmetic  38.6 us (3%)
  between operations  15.3 us (1%)
    dot_general x19, matrix products, ein(): return jnp.einsum(spec, *args, preferred_element_type=f32)  206 us
    reduce_scatter x1, waiting for transfers between devices, body(): lax.psum_scatter(spread(back), AXES, scatter_dimension=0, tiled=True)  166 us
    reduce_scatter x1, waiting for transfers between devices, body(): lax.psum_scatter(spread(w_rows * out), AXES, scatter_dimension=0, tiled=T...  140 us
    ppermute x7, waiting for transfers between devices, body(): lax.ppermute(ring[-1], 'seq', [(dev, (dev + 1) % 8) for dev in range(8)])  115 us
    all_gather x1, waiting for transfers between devices, body(): x_all = lax.all_gather(normed_mid, AXES, axis=0, tiled=True)  102 us
    all_gather x1, waiting for transfers between devices, body(): lax.all_gather(resid_grad.astype(bf16), 'seq', axis=0, tiled=True)  74 us
    unnamed x113, local copies, waits for them, and re-layouts  60.4 us
    unnamed x1, blocking collectives  44.9 us
  transfers between devices with their start and end apart: 19, of which 16 were waited for; matrix products, arithmetic and copies ran while one was open for 15% of the time, Pallas kernels for 0%

profile of v1, /device:TPU:0, one launch (start us, length us, event | category | flops | bytes accessed | tf_op | source)
XLA Modules:
  0.0 1279.2 jit_solution(1104102438059182578)
XLA Ops:
  13.0 30.4 %all_to_all.34 = bf16[8,64,896]{2,1,0:T(8,128)(2,1)S(1)} all-to-all(bf16[8,64,896]{2,1,0:T(8,128)(2,1)S(1)} %copy.233), channel_id=1, replica_groups=mesh['seq'=8,'fsdp'=4] {'seq'}, dimensions={0} | all-to-all | bytes 1835008 | tf_op jit(solution)/shard_map/all_to_all | solution.py:125
  47.5 13.7 %collective-permute-done = bf16[128,2048]{1,0:T(8,128)(2,1)S(1)} collective-permute-done((bf16[128,2048]{1,0:T(8,128)(2,1)S(1)}, bf16[128,2048]{1,0:T(8,128)(2,1)S(1)}, u32[]{:S(2)}, u32[]{:S(2)}) %collective-permute-start) | collective-permute-done | bytes 524320 | tf_op jit(solution)/shard_map/ppermute | solution.py:103
  61.2 13.9 %collective-permute-done.1 = bf16[128,2048]{1,0:T(8,128)(2,1)S(1)} collective-permute-done((bf16[128,2048]{1,0:T(8,128)(2,1)S(1)}, bf16[128,2048]{1,0:T(8,128)(2,1)S(1)}, u32[]{:S(2)}, u32[]{:S(2)}) %collective-permute-start.1) | collective-permute-done | bytes 524320 | tf_op jit(solution)/shard_map/ppermute | solution.py:103
  75.1 13.0 %collective-permute-done.2 = bf16[128,2048]{1,0:T(8,128)(2,1)S(1)} collective-permute-done((bf16[128,2048]{1,0:T(8,128)(2,1)S(1)}, bf16[128,2048]{1,0:T(8,128)(2,1)S(1)}, u32[]{:S(2)}, u32[]{:S(2)}) %collective-permute-start.2) | collective-permute-done | bytes 524320 | tf_op jit(solution)/shard_map/ppermute | solution.py:103
  88.1 17.8 %collective-permute-done.3 = bf16[128,2048]{1,0:T(8,128)(2,1)S(1)} collective-permute-done((bf16[128,2048]{1,0:T(8,128)(2,1)S(1)}, bf16[128,2048]{1,0:T(8,128)(2,1)S(1)}, u32[]{:S(2)}, u32[]{:S(2)}) %collective-permute-start.3) | collective-permute-done | bytes 524320 | tf_op jit(solution)/shard_map/ppermute | solution.py:103
  105.9 22.3 %collective-permute-done.4 = bf16[128,2048]{1,0:T(8,128)(2,1)S(1)} collective-permute-done((bf16[128,2048]{1,0:T(8,128)(2,1)S(1)}, bf16[128,2048]{1,0:T(8,128)(2,1)S(1)}, u32[]{:S(2)}, u32[]{:S(2)}) %collective-permute-start.4) | collective-permute-done | bytes 524320 | tf_op jit(solution)/shard_map/ppermute | solution.py:103
  128.2 12.1 collective-permute-done.5
  140.5 3.2 fusion.80
  143.7 21.9 %collective-permute-done.6 = bf16[128,2048]{1,0:T(8,128)(2,1)} collective-permute-done((bf16[128,2048]{1,0:T(8,128)(2,1)}, bf16[128,2048]{1,0:T(8,128)(2,1)}, u32[]{:S(2)}, u32[]{:S(2)}) %collective-permute-start.6) | collective-permute-done | bytes 524320 | tf_op jit(solution)/shard_map/ppermute | solution.py:103
  171.7 3.4 copy-done.12
  176.0 2.8 copy.235
  180.1 1.7 copy-done.13
  181.9 3.8 fusion.30
  190.6 2.1 fusion.97
  192.7 2.4 copy.296
  196.3 3.5 subtract_convert_fusion.3
  199.9 9.1 fusion.8
  209.0 4.4 fusion.36
  214.3 25.3 %all_to_all.35 = bf16[8,128,256]{1,2,0:T(8,128)(2,1)S(1)} all-to-all(bf16[8,128,256]{1,2,0:T(8,128)(2,1)S(1)} %copy.241), channel_id=1, replica_groups=mesh['seq'=8,'fsdp'=4] {'seq'}, dimensions={0} | all-to-all | bytes 1048576 | tf_op jit(solution)/shard_map/all_to_all | solution.py:148
  239.5 4.8 multiply_reduce_fusion.3
  246.3 43.5 %all-gather.1 = s32[1,4096,8]{1,2,0:T(8,128)S(1)} all-gather(s32[1,128,8]{1,2,0:T(8,128)S(1)} %copy-done.29), channel_id=3, replica_groups=mesh['seq'=8,'fsdp'=4] {'seq','fsdp'}, dimensions={1}, use_global_device_ids=true | all-gather | bytes 135168 | tf_op jit(solution)/shard_map/all_gather | solution.py:100
  290.1 12.5 all-gather.17.cloned.1.call-done
  302.6 7.0 convolution_bitcast_fusion
  309.7 6.2 copy.247
  315.9 102.1 %all-gather.11.cloned.1.call-done = bf16[4096,2048]{1,0:T(8,128)(2,1)} async-done(((bf16[128,2048]{1,0:T(8,128)(2,1)}), bf16[4096,2048]{1,0:T(8,128)(2,1)}) %all-gather.11.cloned.1.call-update) | async-done | bytes 16777232 | tf_op jit(solution)/shard_map/all_gather | solution.py:152
  418.0 9.4 convert_bitcast_fusion
  427.3 8.3 copy.245
  435.6 15.8 %fusion.100 = f32[2,1024,2,512]{3,1,2,0:T(8,128)} fusion(bf16[2,1024,2048,1]{2,1,3,0:T(8,128)(2,1)} %bitcast.244, bf16[2,2,2048,512]{3,2,1,0:T(8,128)(2,1)} %bitcast.293), kind=kOutput, calls=%fused_computation.199 | convolution fusion | flops 8589934592 | bytes 25165824 | tf_op jit(solution)/shard_map/erd,epdf->eprf/dot_general | solution.py:62
  451.4 15.0 %fusion.17 = (bf16[2,2,1024,512]{3,2,1,0:T(8,128)(2,1)S(1)}, f32[2,1024,2,512]{3,1,2,0:T(8,128)}) fusion(f32[2,1024,2,512]{3,1,2,0:T(8,128)} %fusion.100, bf16[2,1024,2048,1]{2,1,3,0:T(8,128)(2,1)S(1)} %bitcast.247, bf16[2,2,2048,512]{3,2,1,0:T(8,128)(2,1)} %bitcast.295), kind=kOutput, calls=%fused_computation.31 | convolution fusion | flops 8602517504 | bytes 37748736 | tf_op jit(solution)/shard_map/erd,epdf->eprf/dot_general | solution.py:62
  466.3 19.9 %fusion.3 = (f32[2,1024]{1,0:T(2,128)S(1)}, f32[2,1024,2048,1]{2,1,3,0:T(8,128)}) fusion(f32[2,32,32,2048]{3,2,1,0:T(8,128)} %copy.247, bf16[2,2,1024,512]{3,2,1,0:T(8,128)(2,1)S(1)} %get-tuple-element.133, bf16[2,2,512,2048]{3,2,1,0:T(8,128)(2,1)} %bitcast.291), kind=kOutput, calls=%fused_computation.8 | convolution fusion | flops 8598321152 | bytes 46145536 | tf_op jit(solution)/shard_map/eprf,epfd->erd/dot_general | solution.py:62
  486.3 11.0 fusion.99
  500.5 17.0 %fusion.2 = (bf16[2,1024,2048]{2,1,0:T(8,128)(2,1)}, bf16[2,1024,2048]{2,1,0:T(8,128)(2,1)}) fusion(f32[2,32,32,2048]{3,2,1,0:T(8,128)} %copy.247, f32[2,1024]{1,0:T(2,128)S(1)} %mul.571, f32[2,1024,2048,1]{2,1,3,0:T(8,128)} %get-tuple-element.136), kind=kLoop, calls=%fused_computation.7 | loop fusion | flops 16777216 | bytes 50339840 | tf_op jit(solution)/shard_map/convert_element_type | solution.py:171
  517.5 18.7 %fusion.16 = (bf16[2,2,1024,512]{3,2,1,0:T(8,128)(2,1)}, bf16[2,2,1024,512]{3,2,1,0:T(8,128)(2,1)S(1)}) fusion(f32[2,1024,2,512]{3,1,2,0:T(8,128)} %fusion.100, f32[2,1024,2,512]{3,1,2,0:T(8,128)} %get-tuple-element.134, bf16[2,2,512,2048]{3,2,1,0:T(8,128)(2,1)} %bitcast.292, bf16[2,1024,2048]{2,1,0:T(8,128)(2,1)} %get-tuple-element.122), kind=kOutput, calls=%fused_computation.29 | convolution fusion | flops 8617197568 | bytes 41943040 | tf_op jit(solution)/shard_map/erd,epfd->eprf/dot_general | solution.py:62
  536.2 16.2 %fusion.101 = f32[2,1024,2048,1]{2,1,3,0:T(8,128)} fusion(bf16[2,2,1024,512]{3,2,1,0:T(8,128)(2,1)S(1)} %get-tuple-element.98, bf16[2,2,2048,512]{3,2,1,0:T(8,128)(2,1)} %bitcast.294), kind=kOutput, calls=%fused_computation.200 | convolution fusion | flops 8589934592 | bytes 29360128 | tf_op jit(solution)/shard_map/eprf,epdf->erd/dot_general | solution.py:62
  552.4 16.9 %fusion.1 = bf16[2,1024,2048]{2,1,0:T(8,128)(2,1)} fusion(f32[2,1024,2048,1]{2,1,3,0:T(8,128)} %fusion.101, bf16[2,2,1024,512]{3,2,1,0:T(8,128)(2,1)} %get-tuple-element.97, bf16[2,2,2048,512]{3,2,1,0:T(8,128)(2,1)} %bitcast.296), kind=kOutput, calls=%fused_computation.4 | convolution fusion | flops 8598323200 | bytes 37748736 | tf_op jit(solution)/shard_map/eprf,epdf->erd/dot_general | solution.py:62
  569.3 10.7 bitcast_convert_fusion
  582.5 2.8 all-to-all-start.2
  585.4 11.0 all-to-all-done.2
  596.6 166.1 %reduce-scatter.8.cloned.1.call-done = bf16[128,2048]{1,0:T(8,128)(2,1)} async-done(((bf16[4096,2048]{1,0:T(8,128)(2,1)}), bf16[128,2048]{1,0:T(8,128)(2,1)}) %reduce-scatter.8.cloned.1.call-update) | async-done | bytes 524304 | tf_op jit(solution)/shard_map/reduce_scatter | solution.py:191
  762.7 1.8 multiply_reduce_fusion
  765.9 74.0 %all-gather.13.cloned.1.call-done = bf16[1024,2048]{1,0:T(8,128)(2,1)} async-done(((bf16[128,2048]{1,0:T(8,128)(2,1)}), bf16[1024,2048]{1,0:T(8,128)(2,1)}) %all-gather.13.cloned.1.call-update) | async-done | bytes 4194320 | tf_op jit(solution)/shard_map/all_gather | solution.py:216
  840.0 4.1 multiply_reduce_fusion.1
  844.1 5.9 fusion.39
  851.4 2.0 fusion.43
  856.9 2.0 copy.260
  859.9 6.9 fusion.64
  866.9 3.4 copy.262
  870.4 8.0 convolution_convert_fusion
  878.4 11.1 bitcast_convert_fusion.1
  891.0 16.9 %fusion.103 = f32[2,2,512,2048]{3,2,1,0:T(8,128)} fusion(bf16[2,2,1024,512]{3,2,1,0:T(8,128)(2,1)} %copy-done.39, bf16[2,1024,2048,1]{2,1,3,0:T(8,128)(2,1)} %bitcast.245), kind=kOutput, calls=%fused_computation.202 | convolution fusion | flops 8589934592 | bytes 29360128 | tf_op jit(solution)/shard_map/erd,eprf->epdf/dot_general | solution.py:62
  907.9 2.6 fusion.102
  910.5 16.5 %fusion.104 = f32[2,2,512,2048]{3,2,1,0:T(8,128)} fusion(bf16[2,2,1024,512]{3,2,1,0:T(8,128)(2,1)} %get-tuple-element.97, bf16[2,1024,2048,1]{2,1,3,0:T(8,128)(2,1)} %bitcast.246), kind=kOutput, calls=%fused_computation.203 | convolution fusion | flops 8589934592 | bytes 29360128 | tf_op jit(solution)/shard_map/erd,eprf->epdf/dot_general | solution.py:62
  927.8 5.8 all-to-all-start.3
  933.6 16.6 %fusion.9 = f32[2,2,512,2048]{3,2,1,0:T(8,128)} fusion(bf16[2,2,1024,512]{3,2,1,0:T(8,128)(2,1)} %copy-done.38, bf16[2,1024,2048]{2,1,0:T(8,128)(2,1)} %get-tuple-element.122), kind=kOutput, calls=%fused_computation.20 | convolution fusion | flops 8589934592 | bytes 29360128 | tf_op jit(solution)/shard_map/eprf,erd->epfd/dot_general | solution.py:62
  950.2 16.3 %copy.269 = f32[4,2048,512]{2,1,0:T(8,128)} copy(f32[4,2048,512]{1,2,0:T(8,128)} %bitcast.236) | data formatting | bytes 33554432
  966.6 16.4 %copy.270 = f32[4,2048,512]{2,1,0:T(8,128)} copy(f32[4,2048,512]{1,2,0:T(8,128)} %bitcast.237) | data formatting | bytes 33554432
  983.0 42.8 %all_gather.31 = bf16[4096,64]{0,1:T(8,128)(2,1)S(1)} all-gather(bf16[128,64]{0,1:T(8,128)(2,1)S(1)} %multiply_convert_fusion.2), channel_id=1, replica_groups=mesh['seq'=8,'fsdp'=4] {'seq','fsdp'}, dimensions={0}, use_global_device_ids=true | all-gather | bytes 540672 | tf_op jit(solution)/shard_map/all_gather | solution.py:209
  1025.8 2.6 fusion.54
  1028.4 21.4 %reduce-scatter.10.cloned.1.call-done = bf16[128,2048]{1,0:T(8,128)(2,1)} async-done(((bf16[1024,2048]{1,0:T(8,128)(2,1)}), bf16[128,2048]{1,0:T(8,128)(2,1)}) %reduce-scatter.10.cloned.1.call-update) | async-done | bytes 524304 | tf_op jit(solution)/shard_map/reduce_scatter | solution.py:230
  1051.6 44.9 %all-reduce = f32[2,32,64]{2,0,1:T(2,128)S(1)} all-reduce(f32[2,32,64]{2,0,1:T(2,128)S(1)} %pad_maximum_fusion.7), channel_id=8, replica_groups=mesh['seq'=8,'fsdp'=4] {'seq','fsdp'}, use_global_device_ids=true, to_apply=%region_27.28.clone | all-reduce | flops 4096 | bytes 32768
  1097.0 140.3 %reduce-scatter.6.cloned.1.call-done = bf16[128,2048]{1,0:T(8,128)(2,1)} async-done(((bf16[4096,2048]{1,0:T(8,128)(2,1)}), bf16[128,2048]{1,0:T(8,128)(2,1)}) %reduce-scatter.6.cloned.1.call-update) | async-done | bytes 524304 | tf_op jit(solution)/shard_map/reduce_scatter | solution.py:200
  1237.3 2.8 fusion.51
  1240.1 2.6 reshape.357
  1248.0 24.1 %reduce-scatter.14.cloned.1.call-done = f32[64,2048]{1,0:T(8,128)} async-done(((f32[256,2048]{1,0:T(8,128)}), f32[64,2048]{1,0:T(8,128)}) %reduce-scatter.14.cloned.1.call-update) | async-done | bytes 524304 | tf_op jit(solution)/shard_map/reduce_scatter | solution.py:218
  (205 shorter events, 50.6 us)
Async XLA Ops:
  7.2 39.2 %copy-start.2 = (bf16[1,128,2048]{2,1,0:T(8,128)(2,1)S(1)}, bf16[1,128,2048]{2,1,0:T(8,128)(2,1)}, u32[]{:S(2)}) copy-start(bf16[1,128,2048]{2,1,0:T(8,128)(2,1)} %param.13) | copy-start | bytes 1572868
  7.2 168.8 %all-gather.15.cloned.1.call-start = ((), (), s32[]{:S(2)}) async-start(), calls=%async_computation.17 | async-start | bytes 4587520 | tf_op jit(solution)/shard_map/all_gather | solution.py:126
  44.8 194.7 %all-gather.9.cloned.1.call-start = ((), (), s32[]{:S(2)}) async-start(), calls=%async_computation.9 | async-start | bytes 8650752 | tf_op jit(solution)/shard_map/all_gather | solution.py:131
  45.6 257.1 %all-gather.17.cloned.1.call-start = ((), (), s32[]{:S(2)}) async-start(), calls=%async_computation.18 | async-start | bytes 17301504 | tf_op jit(solution)/shard_map/all_gather | solution.py:133
  46.3 371.7 %all-gather.11.cloned.1.call-start = ((), (), s32[]{:S(2)}) async-start(), calls=%async_computation.10 | async-start | bytes 17301504 | tf_op jit(solution)/shard_map/all_gather | solution.py:152
  46.4 14.8 %collective-permute-start = (bf16[128,2048]{1,0:T(8,128)(2,1)S(1)}, bf16[128,2048]{1,0:T(8,128)(2,1)S(1)}, u32[]{:S(2)}, u32[]{:S(2)}) collective-permute-start(bf16[128,2048]{1,0:T(8,128)(2,1)S(1)} %bitcast.235), channel_id=1, source_target_pairs={{0,4},{4,8},{8,12},{12,16},{16,20},{20,24},{24,28},{28,0},{1,5},{5... | collective-permute-start | bytes 1572872 | tf_op jit(solution)/shard_map/ppermute | solution.py:103
  61.2 13.9 %collective-permute-start.1 = (bf16[128,2048]{1,0:T(8,128)(2,1)S(1)}, bf16[128,2048]{1,0:T(8,128)(2,1)S(1)}, u32[]{:S(2)}, u32[]{:S(2)}) collective-permute-start(bf16[128,2048]{1,0:T(8,128)(2,1)S(1)} %collective-permute-done), channel_id=1, source_target_pairs={{0,4},{4,8},{8,12},{12,16},{16,20},{20,24},{24,28},{28,0},{1,5},{5... | collective-permute-start | bytes 1572872 | tf_op jit(solution)/shard_map/ppermute | solution.py:103
  75.1 13.0 %collective-permute-start.2 = (bf16[128,2048]{1,0:T(8,128)(2,1)S(1)}, bf16[128,2048]{1,0:T(8,128)(2,1)S(1)}, u32[]{:S(2)}, u32[]{:S(2)}) collective-permute-start(bf16[128,2048]{1,0:T(8,128)(2,1)S(1)} %collective-permute-done.1), channel_id=1, source_target_pairs={{0,4},{4,8},{8,12},{12,16},{16,20},{20,24},{24,28},{28,0},{1,5},{5... | collective-permute-start | bytes 1572872 | tf_op jit(solution)/shard_map/ppermute | solution.py:103
  88.1 17.8 %collective-permute-start.3 = (bf16[128,2048]{1,0:T(8,128)(2,1)S(1)}, bf16[128,2048]{1,0:T(8,128)(2,1)S(1)}, u32[]{:S(2)}, u32[]{:S(2)}) collective-permute-start(bf16[128,2048]{1,0:T(8,128)(2,1)S(1)} %collective-permute-done.2), channel_id=1, source_target_pairs={{0,4},{4,8},{8,12},{12,16},{16,20},{20,24},{24,28},{28,0},{1,5},{5... | collective-permute-start | bytes 1572872 | tf_op jit(solution)/shard_map/ppermute | solution.py:103
  105.9 22.3 %collective-permute-start.4 = (bf16[128,2048]{1,0:T(8,128)(2,1)S(1)}, bf16[128,2048]{1,0:T(8,128)(2,1)S(1)}, u32[]{:S(2)}, u32[]{:S(2)}) collective-permute-start(bf16[128,2048]{1,0:T(8,128)(2,1)S(1)} %collective-permute-done.3), channel_id=1, source_target_pairs={{0,4},{4,8},{8,12},{12,16},{16,20},{20,24},{24,28},{28,0},{1,5},{5... | collective-permute-start | bytes 1572872 | tf_op jit(solution)/shard_map/ppermute | solution.py:103
  128.2 12.3 copy-start.22
  128.2 12.1 collective-permute-start.5
  140.3 25.4 %collective-permute-start.6 = (bf16[128,2048]{1,0:T(8,128)(2,1)}, bf16[128,2048]{1,0:T(8,128)(2,1)}, u32[]{:S(2)}, u32[]{:S(2)}) collective-permute-start(bf16[128,2048]{1,0:T(8,128)(2,1)} %collective-permute-done.5), channel_id=1, source_target_pairs={{0,4},{4,8},{8,12},{12,16},{16,20},{20,24},{24,28},{28,0},{1,5},{5... | collective-permute-start | bytes 1572872 | tf_op jit(solution)/shard_map/ppermute | solution.py:103
  140.5 30.9 %copy-start.23 = (bf16[128,2048]{1,0:T(8,128)(2,1)S(1)}, bf16[128,2048]{1,0:T(8,128)(2,1)}, u32[]{:S(2)}) copy-start(bf16[128,2048]{1,0:T(8,128)(2,1)} %copy-done.22) | copy-start | bytes 1572868
  143.7 52.6 %copy-start.6 = (f32[1024,64]{1,0:T(8,128)}, f32[1024,64]{1,0:T(8,128)S(1)}, u32[]{:S(2)}) copy-start(f32[1024,64]{1,0:T(8,128)S(1)} %get-tuple-element.126) | copy-start | bytes 786436
  171.7 3.4 copy-start.12
  176.0 3.6 copy-start.33
  176.0 5.8 copy-start.13
  178.8 6.9 copy-start.4
  179.5 0.6 copy-start.27
  179.5 64.8 %copy-start.25 = (f32[2048]{0:T(1024)}, f32[2048]{0:T(1024)S(1)}, u32[]{:S(2)}) copy-start(f32[2048]{0:T(1024)S(1)} %get-tuple-element.84) | copy-start | bytes 24580
  185.8 23.2 %copy-start.10 = (bf16[1024,256]{0,1:T(8,128)(2,1)}, bf16[1024,256]{0,1:T(8,128)(2,1)S(1)}, u32[]{:S(2)}) copy-start(bf16[1024,256]{0,1:T(8,128)(2,1)S(1)} %slice.127) | copy-start | bytes 1572868
  199.9 9.1 copy-start.14
  213.4 0.8 copy-start.20
  239.5 6.8 copy-start.29
  244.3 1.0 copy-start
  244.3 45.5 %copy-start.35 = (f32[128]{0:T(128)}, f32[128]{0:T(128)S(1)}, u32[]{:S(2)}) copy-start(f32[128]{0:T(128)S(1)} %get-tuple-element.129) | copy-start | bytes 1540
  244.3 45.5 %copy-start.31 = (f32[128]{0:T(128)}, f32[128]{0:T(128)S(1)}, u32[]{:S(2)}) copy-start(f32[128]{0:T(128)S(1)} %fusion.88) | copy-start | bytes 1540
  246.2 516.4 %reduce-scatter.8.cloned.1.call-start = ((), (), s32[]{:S(2)}) async-start(), calls=%async_computation.12 | async-start | bytes 17301504 | tf_op jit(solution)/shard_map/reduce_scatter | solution.py:191
  435.6 15.8 %copy-start.5 = (bf16[2,32,32,2048]{3,2,1,0:T(8,128)(2,1)S(1)}, bf16[2,32,32,2048]{3,2,1,0:T(8,128)(2,1)}, u32[]{:S(2)}) copy-start(bf16[2,32,32,2048]{3,2,1,0:T(8,128)(2,1)} %copy.245) | copy-start | bytes 25165828
  466.3 19.9 %copy-start.38 = (bf16[2,2,1024,512]{3,2,1,0:T(8,128)(2,1)}, bf16[2,2,1024,512]{3,2,1,0:T(8,128)(2,1)S(1)}, u32[]{:S(2)}) copy-start(bf16[2,2,1024,512]{3,2,1,0:T(8,128)(2,1)S(1)} %get-tuple-element.133) | copy-start | bytes 12582916
  536.2 16.2 %copy-start.39 = (bf16[2,2,1024,512]{3,2,1,0:T(8,128)(2,1)}, bf16[2,2,1024,512]{3,2,1,0:T(8,128)(2,1)S(1)}, u32[]{:S(2)}) copy-start(bf16[2,2,1024,512]{3,2,1,0:T(8,128)(2,1)S(1)} %get-tuple-element.98) | copy-start | bytes 12582916
  580.0 1.0 copy-start.8
  580.0 16.3 %copy-start.30 = (s32[1,128,8]{1,2,0:T(8,128)S(1)}, s32[1,128,8]{1,2,0:T(8,128)}, u32[]{:S(2)}) copy-start(s32[1,128,8]{1,2,0:T(8,128)} %param.15) | copy-start | bytes 12292
  580.0 182.6 %copy-start.1 = (f32[128,2048]{1,0:T(8,128)S(1)}, f32[128,2048]{1,0:T(8,128)}, u32[]{:S(2)}) copy-start(f32[128,2048]{1,0:T(8,128)} %copy-done) | copy-start | bytes 3145732
  580.0 182.6 %copy-start.26 = (f32[2048]{0:T(1024)S(1)}, f32[2048]{0:T(1024)}, u32[]{:S(2)}) copy-start(f32[2048]{0:T(1024)} %copy-done.25) | copy-start | bytes 24580
  580.1 182.6 %copy-start.32 = (f32[128]{0:T(128)S(1)}, f32[128]{0:T(128)}, u32[]{:S(2)}) copy-start(f32[128]{0:T(128)} %copy-done.31) | copy-start | bytes 1540
  580.1 184.4 %copy-start.36 = (f32[128]{0:T(128)S(1)}, f32[128]{0:T(128)}, u32[]{:S(2)}) copy-start(f32[128]{0:T(128)} %copy-done.35) | copy-start | bytes 1540
  580.1 184.4 %copy-start.9 = (bf16[1,128,2048]{2,1,0:T(8,128)(2,1)S(1)}, bf16[1,128,2048]{2,1,0:T(8,128)(2,1)}, u32[]{:S(2)}) copy-start(bf16[1,128,2048]{2,1,0:T(8,128)(2,1)} %param.14) | copy-start | bytes 1572868
  582.5 13.9 %all-to-all-start.2 = ((f32[32,2,128]{2,1,0:T(2,128)}), f32[32,2,128]{2,1,0:T(2,128)S(1)}, u32[]{:S(2)}, u32[]{:S(2)}) async-start(f32[32,2,128]{2,1,0:T(2,128)} %get-tuple-element.92), calls=%async_computation.4 | async-start | bytes 65536 | tf_op jit(solution)/shard_map/all_to_all | solution.py:196
  585.3 254.7 %all-gather.13.cloned.1.call-start = ((), (), s32[]{:S(2)}) async-start(), calls=%async_computation.13 | async-start | bytes 4718592 | tf_op jit(solution)/shard_map/all_gather | solution.py:216
  765.7 162.2 %reduce-scatter.12.cloned.1.call-start = ((), (), s32[]{:S(2)}) async-start(), calls=%async_computation.15 | async-start | bytes 7864320 | tf_op jit(solution)/shard_map/reduce_scatter | solution.py:235
  765.9 84.0 %copy-start.11 = (bf16[1024,256]{0,1:T(8,128)(2,1)S(1)}, bf16[1024,256]{0,1:T(8,128)(2,1)}, u32[]{:S(2)}) copy-start(bf16[1024,256]{0,1:T(8,128)(2,1)} %copy-done.10) | copy-start | bytes 1572868
  840.0 9.9 slice-start
  844.0 5.9 slice-start.1
  849.9 1.4 copy-start.17
  849.9 1.4 copy-start.18
  850.0 3.4 copy-start.15
  850.0 3.4 copy-start.16
  851.3 3.4 copy-start.7
  851.4 3.4 copy-start.19
  853.4 6.5 copy-start.28
  853.4 6.5 copy-start.34
  866.9 3.5 copy-start.24
  870.3 179.6 %reduce-scatter.10.cloned.1.call-start = ((), (), s32[]{:S(2)}) async-start(), calls=%async_computation.14 | async-start | bytes 4718592 | tf_op jit(solution)/shard_map/reduce_scatter | solution.py:230
  878.4 358.9 %reduce-scatter.6.cloned.1.call-start = ((), (), s32[]{:S(2)}) async-start(), calls=%async_computation.11 | async-start | bytes 17301504 | tf_op jit(solution)/shard_map/reduce_scatter | solution.py:200
  889.5 1.2 copy-start.3
  889.6 382.6 %reduce-scatter.14.cloned.1.call-start = ((), (), s32[]{:S(2)}) async-start(), calls=%async_computation.16 | async-start | bytes 2621440 | tf_op jit(solution)/shard_map/reduce_scatter | solution.py:218
  890.9 16.9 %copy-start.21 = (bf16[2,128,1024]{2,1,0:T(8,128)(2,1)S(1)}, bf16[2,128,1024]{2,1,0:T(8,128)(2,1)}, u32[]{:S(2)}) copy-start(bf16[2,128,1024]{2,1,0:T(8,128)(2,1)} %copy-done.20) | copy-start | bytes 1572868
  890.9 16.9 %copy-start.37 = (bf16[1024,2048]{1,0:T(8,128)(2,1)S(1)}, bf16[1024,2048]{1,0:T(8,128)(2,1)}, u32[]{:S(2)}) copy-start(bf16[1024,2048]{1,0:T(8,128)(2,1)} %all-gather.13.cloned.1.call-done) | copy-start | bytes 12582916
  927.8 312.3 %all-to-all-start.3 = ((f32[8,64,768]{2,1,0:T(8,128)}), f32[8,64,768]{2,1,0:T(8,128)}, u32[]{:S(2)}, u32[]{:S(2)}) async-start(f32[8,64,768]{2,1,0:T(8,128)} %bitcast.266), calls=%async_computation.7 | async-start | bytes 3145728 | tf_op jit(solution)/shard_map/all_to_all | solution.py:236
Sparse Core Ops, SparseCore 0:
  44.9 30.1 all-gather.14
  78.0 96.8 all-gather.8
  177.8 124.8 all-gather.16
  305.4 112.5 all-gather.10
  580.2 182.3 reduce-scatter.7
  765.8 74.1 all-gather.12
  870.4 57.3 reduce-scatter.11
  931.5 118.3 reduce-scatter.9
  1052.2 185.0 reduce-scatter.5
  1240.2 31.8 reduce-scatter.13
